TPU v7x, 32 devices: a whole 2x2x4 slice. The times are simulated.
32 devices in a mesh: scan: 2 (over y), ang: 4 (over z), row: 4 (over x, core).
Axes of the slice: x: 2, y: 2, z: 4, core: 2. Of those that a mesh axis runs over, the one named last changes fastest.
Arguments:
- projections: bfloat16 [8, 32, 2560], P(('scan', 'ang'), 'row'), parts along dimension 0, may hold values from 0 to 2
- flats: float32 [64, 2560], P(('scan', 'row')), parts along dimension 0, may hold values from 1 to 3
- block_start: int32 [4, 4], replicated, may hold values from 0 to 2528
- bp_weights: bfloat16 [4, 32, 1024], P(None, None, 'ang'), may hold values from -0.5 to 0.5
Outputs:
- recon: float32 [64, 1024], P(('scan', 'row'), 'ang'), parts along dimension 0
There are 2 independent parts, one for each index of `scan`. A program takes and returns all parts, laid end to end along the dimension named above; an argument that names none is the same for every part. Nothing has to cross between parts.
Inputs may be any that keep to these rules, and one draw needn't show every extreme that they name: block_start[a, r] is the first of the 32 detector columns that pixel region r reads at angle a.
All inputs are finite; a program needn't handle non-finite values.
Results may differ from a plain program's by a relative error of at most 0.009.
Values may be sent and summed in bfloat16 or wider, within the bound.
No kernel may reach another device: no remote copies, remote signals or barrier semaphores. Data moves between devices by JAX's collectives and lax.ppermute only.
A program may use at most 64 MiB of HBM per device.

v0:
```python
import jax
import jax.numpy as jnp
from jax import lax
from jax.sharding import PartitionSpec as P

HALO = 4


paganin_beta = 8.0
ramp_gain = 320.0
highest = lax.Precision.HIGHEST


def with_halo(x, sides, width):
    for axis, dim in sides:
        peers, length = (lax.axis_size(axis), x.shape[dim])
        up = [(i, (i + 1) % peers) for i in range(peers - 1)]
        down = [(j, i) for i, j in up]
        last = lax.slice_in_dim(x, length - width, length, axis=dim)
        initial = lax.slice_in_dim(x, 0, width, axis=dim)
        before = lax.ppermute(last, axis, up)
        after = lax.ppermute(initial, axis, down)
        x = jnp.concatenate([before, x, after], axis=dim)
    return x


def contract(form, left, right):
    return jnp.einsum(form, left, right, precision=highest)


def circle_table(count):
    index = jnp.arange(count, dtype=jnp.int32)
    phase = index[:, None] * index[None, :] % count
    angle = 2.0 * jnp.pi / count * phase.astype(jnp.float32)
    return (jnp.cos(angle), jnp.sin(angle))


def twiddle_table(blocks, width):
    first = jnp.arange(blocks, dtype=jnp.int32)
    second = jnp.arange(128, dtype=jnp.int32)
    phase = first[:, None] * second[None, :] % width
    angle = 2.0 * jnp.pi / width * phase.astype(jnp.float32)
    return (jnp.cos(angle), jnp.sin(angle))


def columns_forward(values, tables):
    outer_cos, outer_sin, turn_cos, turn_sin, inner_cos, inner_sin = tables
    first_re = contract("...ab,ak->...kb", values, outer_cos)
    first_im = -contract("...ab,ak->...kb", values, outer_sin)
    turned_re = first_re * turn_cos + first_im * turn_sin
    turned_im = first_im * turn_cos - first_re * turn_sin
    spec_re = contract("...kb,bm->...km", turned_re, inner_cos) + contract(
        "...kb,bm->...km", turned_im, inner_sin
    )
    spec_im = contract("...kb,bm->...km", turned_im, inner_cos) - contract(
        "...kb,bm->...km", turned_re, inner_sin
    )
    return (spec_re, spec_im)


def columns_inverse(spec_re, spec_im, tables):
    outer_cos, outer_sin, turn_cos, turn_sin, inner_cos, inner_sin = tables
    back_re = contract("...km,bm->...kb", spec_re, inner_cos) - contract(
        "...km,bm->...kb", spec_im, inner_sin
    )
    back_im = contract("...km,bm->...kb", spec_im, inner_cos) + contract(
        "...km,bm->...kb", spec_re, inner_sin
    )
    untwist_re = back_re * turn_cos - back_im * turn_sin
    untwist_im = back_im * turn_cos + back_re * turn_sin
    values = contract("...kb,ak->...ab", untwist_re, outer_cos) - contract(
        "...kb,ak->...ab", untwist_im, outer_sin
    )
    return values / (outer_cos.shape[0] * 128)


def body(projections, flats, block_start, bp_weights):
    angles_dev, rows_dev, width = projections.shape
    blocks_count = width // 128
    tile_rows = rows_dev + 2 * HALO
    cb_width = bp_weights.shape[1]
    outer_cos, outer_sin = circle_table(blocks_count)
    turn_cos, turn_sin = twiddle_table(blocks_count, width)
    inner_cos, inner_sin = circle_table(128)
    tables = (outer_cos, outer_sin, turn_cos, turn_sin, inner_cos, inner_sin)
    row_cos, row_sin = circle_table(tile_rows)
    freq_index = (
        jnp.arange(blocks_count, dtype=jnp.int32)[:, None]
        + blocks_count * jnp.arange(128, dtype=jnp.int32)[None, :]
    )
    col_freq = freq_index.astype(jnp.float32)
    row_freq = jnp.arange(tile_rows, dtype=jnp.float32)
    lam = (4.0 * jnp.sin(jnp.pi * row_freq / tile_rows) ** 2)[:, None, None] + (
        4.0 * jnp.sin(jnp.pi * col_freq / width) ** 2
    )[None, :, :]
    filt = 1.0 / (1.0 + paganin_beta * lam)
    folded = jnp.minimum(col_freq, width - col_freq)
    ramp = ramp_gain * (folded / width) * (0.5 + 0.5 * jnp.cos(2.0 * jnp.pi * folded / width))
    contrast = 1.0 - projections.astype(jnp.float32) / flats[None, :, :]
    shaped = contrast.reshape(angles_dev, rows_dev, blocks_count, 128)
    widened = with_halo(shaped.astype(jnp.bfloat16), (("row", 1),), HALO).astype(shaped.dtype)
    spec_re, spec_im = columns_forward(widened, tables)
    rows_re = contract("tk,atbm->akbm", row_cos, spec_re) + contract(
        "tk,atbm->akbm", row_sin, spec_im
    )
    rows_im = contract("tk,atbm->akbm", row_cos, spec_im) - contract(
        "tk,atbm->akbm", row_sin, spec_re
    )
    rows_re = rows_re * filt
    rows_im = rows_im * filt
    inner_rcos = row_cos[HALO : HALO + rows_dev]
    inner_rsin = row_sin[HALO : HALO + rows_dev]
    kept_re = (
        contract("tk,akbm->atbm", inner_rcos, rows_re)
        - contract("tk,akbm->atbm", inner_rsin, rows_im)
    ) / tile_rows
    kept_im = (
        contract("tk,akbm->atbm", inner_rcos, rows_im)
        + contract("tk,akbm->atbm", inner_rsin, rows_re)
    ) / tile_rows
    filtered = columns_inverse(kept_re * ramp, kept_im * ramp, tables)
    sinogram = filtered.reshape(angles_dev, rows_dev, width).astype(jnp.bfloat16)
    region = lax.axis_index("ang")

    def cut_block(sheet, begin):
        return lax.dynamic_slice(sheet, (0, begin), (rows_dev, cb_width))

    my_column = lax.dynamic_index_in_dim(block_start, region, 1, keepdims=False)
    blocks = jax.vmap(cut_block)(lax.all_gather(sinogram, "ang", axis=0, tiled=True), my_column)
    return jnp.einsum("arc,acp->rp", blocks, bp_weights, preferred_element_type=jnp.float32)


def solution(mesh):
    placed = (P(("scan", "ang"), "row", None), P(("scan", "row"), None), P(), P(None, None, "ang"))
    return jax.shard_map(
        body, mesh=mesh, in_specs=placed, out_specs=P(("scan", "row"), "ang"), check_vma=False
    )
```

profile of v0, /device:TPU:0, one launch (start us, length us, event | category | flops | bytes accessed | tf_op | source)
XLA Modules:
  0.0 33.9 jit_solution(8301812078791457497)
XLA Ops:
  0.0 0.9 %fusion.61 = bf16[1,8,20,128]{3,1,2,0:T(8,128)(2,1)S(1)} fusion(f32[8,2560]{1,0:T(8,128)} %param.5, bf16[1,8,2560]{2,1,0:T(8,128)(2,1)} %param.4), kind=kLoop, calls=%fused_computation.82 | loop fusion | flops 81920 | bytes 163840 | tf_op jit(solution)/shard_map/convert_element_type | solution.py:101
  1.0 2.4 %collective-permute-start = (bf16[1,4,20,128]{3,2,1,0:T(8,128)(2,1)S(1)}, bf16[1,4,20,128]{3,2,1,0:T(8,128)(2,1)S(1)}, u32[]{:S(2)}, u32[]{:S(2)}) collective-permute-start(bf16[1,4,20,128]{3,2,1,0:T(8,128)(2,1)S(1)} %get-tuple-element.5), channel_id=1, source_target_pairs={{0,1},{1,2},{2,3},{4,5},{5,6},{6,7},{8,9},{9,10},{10,11},{12,13},{... | collective-permute-start | bytes 61448 | tf_op jit(solution)/shard_map/ppermute | solution.py:21
  3.4 1.3 %collective-permute-start.1 = (bf16[1,4,20,128]{3,2,1,0:T(8,128)(2,1)S(1)}, bf16[1,4,20,128]{3,2,1,0:T(8,128)(2,1)S(1)}, u32[]{:S(2)}, u32[]{:S(2)}) collective-permute-start(bf16[1,4,20,128]{3,2,1,0:T(8,128)(2,1)S(1)} %get-tuple-element.6), channel_id=1, source_target_pairs={{1,0},{2,1},{3,2},{5,4},{6,5},{7,6},{9,8},{10,9},{11,10},{13,12},{... | collective-permute-start | bytes 61448 | tf_op jit(solution)/shard_map/ppermute | solution.py:22
  4.7 0.1 fusion.83
  4.8 0.1 fusion.118
  4.9 0.1 multiply_multiply_fusion
  5.1 0.9 %fusion.128 = s32[4]{0:T(128)S(1)} fusion(s32[4,4]{1,0:T(4,128)} %param.6, s32[]{:T(128)S(6)} %select_n.92), kind=kLoop, calls=%fused_computation.143 | loop fusion | flops 32 | bytes 36 | tf_op jit(solution)/shard_map/vmap()/gather | solution.py:126
  5.9 2.6 %collective-permute-done.1 = bf16[1,4,20,128]{3,2,1,0:T(8,128)(2,1)S(1)} collective-permute-done((bf16[1,4,20,128]{3,2,1,0:T(8,128)(2,1)S(1)}, bf16[1,4,20,128]{3,2,1,0:T(8,128)(2,1)S(1)}, u32[]{:S(2)}, u32[]{:S(2)}) %collective-permute-start.1) | collective-permute-done | bytes 20512 | tf_op jit(solution)/shard_map/ppermute | solution.py:22
  8.6 0.4 %fusion = f32[20,1,16,128]{3,0,2,1:T(8,128)S(1)} fusion(bf16[1,4,20,128]{3,2,1,0:T(8,128)(2,1)S(1)} %collective-permute-done.1, bf16[1,8,20,128]{3,2,1,0:T(8,128)(2,1)S(1)} %copy.40, bf16[1,4,20,128]{3,2,1,0:T(8,128)(2,1)S(1)} %collective-permute-done), kind=kOutput, calls=%fused_computation.4 | convolution fusion | flops 10120720 | bytes 245760 | tf_op jit(solution)/shard_map/...ab,ak->...kb/dot_general | solution.py:28
  8.9 0.4 %convolution_bitcast_fusion = f32[20,1,16,128]{3,0,2,1:T(8,128)S(1)} fusion(bf16[1,4,20,128]{3,2,1,0:T(8,128)(2,1)S(1)} %collective-permute-done.1, bf16[1,8,20,128]{3,2,1,0:T(8,128)(2,1)S(1)} %copy.40, bf16[1,4,20,128]{3,2,1,0:T(8,128)(2,1)S(1)} %collective-permute-done), kind=kOutput, calls=%fused_computation.5 | convolution fusion | flops 10079760 | bytes 245760 | tf_op jit(solution)/shard_map/...ab,ak->...kb/dot_general | solution.py:28
  9.3 0.6 %fusion.17 = f32[16,20,128]{2,1,0:T(8,128)S(1)} fusion(f32[20,1,16,128]{3,0,2,1:T(8,128)S(1)} %fusion, f32[20,1,16,128]{3,0,2,1:T(8,128)S(1)} %convolution_bitcast_fusion, f32[20,128]{1,0:T(8,128)S(1)} %get-tuple-element.9, f32[20,128]{1,0:T(8,128)S(1)} %get-tuple-element.10), kind=kOutput, calls=%fused_computation.30 | convolution fusion | flops 63266816 | bytes 512000 | tf_op jit(solution)/shard_map/...kb,bm->...km/dot_general | solution.py:28
  9.9 0.6 %fusion.19 = f32[16,20,128]{2,1,0:T(8,128)S(1)} fusion(f32[20,1,16,128]{3,0,2,1:T(8,128)S(1)} %convolution_bitcast_fusion, f32[20,1,16,128]{3,0,2,1:T(8,128)S(1)} %fusion, f32[20,128]{1,0:T(8,128)S(1)} %get-tuple-element.9, f32[20,128]{1,0:T(8,128)S(1)} %get-tuple-element.10), kind=kOutput, calls=%fused_computation.32 | convolution fusion | flops 63266816 | bytes 512000 | tf_op jit(solution)/shard_map/...kb,bm->...km/dot_general | solution.py:28
  10.4 0.6 %convolution_add_fusion = f32[16,20,128]{2,1,0:T(8,128)S(1)} fusion(f32[16,20,128]{2,1,0:T(8,128)S(1)} %fusion.17, f32[20,1,16,128]{3,0,2,1:T(8,128)S(1)} %convolution_bitcast_fusion, f32[20,1,16,128]{3,0,2,1:T(8,128)S(1)} %fusion, f32[20,128]{1,0:T(8,128)S(1)} %get-tuple-element.9, f32[20,128]{1,0:T(8,128)S(1)} %get-tuple-element.10), kind=kOutput, calls=%fused_computation.2 | convolution fusion | flops 63307776 | bytes 675840 | tf_op jit(solution)/shard_map/...kb,bm->...km/dot_general | solution.py:28
  11.0 0.4 %fusion.26 = f32[20,128,16]{1,2,0:T(8,128)S(1)} fusion(f32[16,20,128]{2,1,0:T(8,128)S(1)} %convolution_add_fusion), kind=kOutput, calls=%fused_computation.42 | convolution fusion | flops 7867904 | bytes 327680 | tf_op jit(solution)/shard_map/tk,atbm->akbm/dot_general | solution.py:28
  11.4 0.6 %convolution_subtract_fusion = f32[16,20,128]{2,1,0:T(8,128)S(1)} fusion(f32[16,20,128]{2,1,0:T(8,128)S(1)} %fusion.19, f32[20,1,16,128]{3,0,2,1:T(8,128)S(1)} %fusion, f32[20,1,16,128]{3,0,2,1:T(8,128)S(1)} %convolution_bitcast_fusion, f32[20,128]{1,0:T(8,128)S(1)} %get-tuple-element.9, f32[20,128]{1,0:T(8,128)S(1)} %get-tuple-element.10), kind=kOutput, calls=%fused_computation.1 | convolution fusion | flops 63307776 | bytes 675840 | tf_op jit(solution)/shard_map/...kb,bm->...km/dot_general | solution.py:28
  12.0 0.4 %fusion.22 = f32[20,128,16]{1,2,0:T(8,128)S(1)} fusion(f32[16,20,128]{2,1,0:T(8,128)S(1)} %convolution_subtract_fusion), kind=kOutput, calls=%fused_computation.38 | convolution fusion | flops 7867904 | bytes 327680 | tf_op jit(solution)/shard_map/tk,atbm->akbm/dot_general | solution.py:28
  12.4 0.4 %fusion.4 = f32[16,20,128]{2,0,1:T(8,128)S(1)} fusion(f32[20,128,16]{1,2,0:T(8,128)S(1)} %fusion.26, f32[16,20,128]{2,1,0:T(8,128)S(1)} %convolution_subtract_fusion, f32[20,128]{1,0:T(8,128)S(1)} %get-tuple-element.8, f32[16]{0:T(128)S(1)} %multiply_multiply_fusion.2), kind=kOutput, calls=%fused_computation.11 | convolution fusion | flops 8113664 | bytes 501824 | tf_op jit(solution)/shard_map/tk,atbm->akbm/dot_general | solution.py:28
  12.8 0.4 %fusion.6 = f32[16,20,128]{2,0,1:T(8,128)S(1)} fusion(f32[20,128,16]{1,2,0:T(8,128)S(1)} %fusion.22, f32[16,20,128]{2,1,0:T(8,128)S(1)} %convolution_add_fusion, f32[20,128]{1,0:T(8,128)S(1)} %get-tuple-element.8, f32[16]{0:T(128)S(1)} %multiply_multiply_fusion.2), kind=kOutput, calls=%fused_computation.13 | convolution fusion | flops 8113664 | bytes 501824 | tf_op jit(solution)/shard_map/tk,atbm->akbm/dot_general | solution.py:28
  13.2 0.2 fusion.124
  13.4 0.2 fusion.123
  13.7 0.2 fusion.12
  13.9 0.5 %fusion.32 = f32[8,20,128]{2,1,0:T(8,128)S(1)} fusion(f32[8,20,128]{2,0,1:T(8,128)S(1)} %fusion.12), kind=kOutput, calls=%fused_computation.48 | convolution fusion | flops 31686656 | bytes 163840 | tf_op jit(solution)/shard_map/...km,bm->...kb/dot_general | solution.py:28
  14.4 0.2 fusion.14
  14.6 0.5 %fusion.28 = f32[8,20,128]{2,1,0:T(8,128)S(1)} fusion(f32[8,20,128]{2,0,1:T(8,128)S(1)} %fusion.14), kind=kOutput, calls=%fused_computation.44 | convolution fusion | flops 31686656 | bytes 163840 | tf_op jit(solution)/shard_map/...km,bm->...kb/dot_general | solution.py:28
  15.1 0.5 %convolution_subtract_fusion.3 = f32[8,20,128]{2,1,0:T(8,128)S(1)} fusion(f32[8,20,128]{2,1,0:T(8,128)S(1)} %fusion.32, f32[8,20,128]{2,0,1:T(8,128)S(1)} %fusion.14), kind=kOutput, calls=%fused_computation.17 | convolution fusion | flops 31707136 | bytes 245760 | tf_op jit(solution)/shard_map/...km,bm->...kb/dot_general | solution.py:28
  15.6 0.5 %convolution_add_fusion.2 = f32[8,20,128]{2,1,0:T(8,128)S(1)} fusion(f32[8,20,128]{2,1,0:T(8,128)S(1)} %fusion.28, f32[8,20,128]{2,0,1:T(8,128)S(1)} %fusion.12), kind=kOutput, calls=%fused_computation.16 | convolution fusion | flops 31707136 | bytes 245760 | tf_op jit(solution)/shard_map/...km,bm->...kb/dot_general | solution.py:28
  16.1 0.3 fusion.37
  16.5 0.3 fusion.15
  16.8 14.0 %all_gather.3 = bf16[4,8,2560]{2,1,0:T(8,128)(2,1)S(1)} all-gather(bf16[1,8,2560]{2,1,0:T(8,128)(2,1)S(1)} %convert_element_type.129), channel_id=1, replica_groups=mesh['scan'=2,'ang'=4,'row'=4] {'ang'}, dimensions={0}, use_global_device_ids=true | all-gather | bytes 204800 | tf_op jit(solution)/shard_map/all_gather | solution.py:129
  30.8 1.5 %copy.57 = bf16[4,8,2560]{1,0,2:T(4,128)(2,1)S(1)} copy(bf16[4,8,2560]{2,1,0:T(8,128)(2,1)S(1)} %all_gather.3) | data formatting | bytes 327680 | tf_op jit(solution)/shard_map/all_gather | solution.py:129
  32.3 0.7 %gather_fusion = bf16[4,8,32]{1,0,2:T(4,128)(2,1)S(1)} fusion(bf16[4,8,2560]{1,0,2:T(4,128)(2,1)S(1)} %copy.57, s32[4]{0:T(128)S(1)} %fusion.128), kind=kCustom, calls=%fused_computation | custom fusion | bytes 4144 | tf_op jit(solution)/shard_map/vmap()/gather | solution.py:126
  33.1 0.8 %convolution_bitcast_fusion.1 = f32[8,256]{1,0:T(8,128)} fusion(bf16[4,32,256]{2,1,0:T(8,128)(2,1)S(1)} %copy-done, bf16[4,8,32]{1,0,2:T(4,128)(2,1)S(1)} %gather_fusion), kind=kOutput, calls=%fused_computation.28 | convolution fusion | flops 524288 | bytes 75776 | tf_op jit(solution)/shard_map/arc,acp->rp/dot_general | solution.py:130
  (9 shorter events, 0.2 us)
Async XLA Ops:
  0.0 33.1 %copy-start = (bf16[4,32,256]{2,1,0:T(8,128)(2,1)S(1)}, bf16[4,32,256]{2,1,0:T(8,128)(2,1)}, u32[]{:S(2)}) copy-start(bf16[4,32,256]{2,1,0:T(8,128)(2,1)} %param.7) | copy-start | bytes 196612
  1.0 5.0 %collective-permute-start = (bf16[1,4,20,128]{3,2,1,0:T(8,128)(2,1)S(1)}, bf16[1,4,20,128]{3,2,1,0:T(8,128)(2,1)S(1)}, u32[]{:S(2)}, u32[]{:S(2)}) collective-permute-start(bf16[1,4,20,128]{3,2,1,0:T(8,128)(2,1)S(1)} %get-tuple-element.5), channel_id=1, source_target_pairs={{0,1},{1,2},{2,3},{4,5},{5,6},{6,7},{8,9},{9,10},{10,11},{12,13},{... | collective-permute-start | bytes 61448 | tf_op jit(solution)/shard_map/ppermute | solution.py:21
  3.4 5.2 %collective-permute-start.1 = (bf16[1,4,20,128]{3,2,1,0:T(8,128)(2,1)S(1)}, bf16[1,4,20,128]{3,2,1,0:T(8,128)(2,1)S(1)}, u32[]{:S(2)}, u32[]{:S(2)}) collective-permute-start(bf16[1,4,20,128]{3,2,1,0:T(8,128)(2,1)S(1)} %get-tuple-element.6), channel_id=1, source_target_pairs={{1,0},{2,1},{3,2},{5,4},{6,5},{7,6},{9,8},{10,9},{11,10},{13,12},{... | collective-permute-start | bytes 61448 | tf_op jit(solution)/shard_map/ppermute | solution.py:22
where the time goes:
time: 34.1 us; the launch traced here: 33.9 us
  blocking collectives  14 us (41%)
  matrix products  8.87 us (26%)
  starting transfers between devices  3.69 us (11%)
  waiting for transfers between devices  2.63 us (8%)
  local copies, waits for them, and re-layouts  2.31 us (7%)
  other arithmetic  2.17 us (6%)
    all_gather x1, blocking collectives, body(): lax.all_gather(sinogram, 'ang', axis=0, tiled=True)  14 us
    dot_general x20, matrix products, contract(): return jnp.einsum(form, left, right, precision=highest)  8.09 us
    ppermute x1, waiting for transfers between devices, with_halo(): after = lax.ppermute(initial, axis, down)  2.63 us
    ppermute x1, starting transfers between devices, with_halo(): before = lax.ppermute(last, axis, up)  2.4 us
    all_gather x1, local copies, waits for them, and re-layouts, body(): lax.all_gather(sinogram, 'ang', axis=0, tiled=True)  1.5 us
    ppermute x1, starting transfers between devices, with_halo(): after = lax.ppermute(initial, axis, down)  1.29 us
    convert_element_type x1, other arithmetic, body(): shaped.astype(jnp.bfloat16)  0.94 us
    gather x1, other arithmetic, cut_block(): return lax.dynamic_slice(sheet, (0, begin), (rows_dev, cb_width))  0.87 us
  transfers between devices with their start and end apart: 2, of which 1 were waited for; matrix products, arithmetic and copies ran while one was open for 4% of the time, Pallas kernels for 0%

commit v1 on v0

v1 whole, which is shorter than its diff:
```python
import functools

import jax
import jax.numpy as jnp
import numpy as np
from jax import lax
from jax.experimental import pallas as pl
from jax.experimental.pallas import tpu as pltpu
from jax.sharding import PartitionSpec as P

HALO = 4
LANES = 128
paganin_beta = 8.0
ramp_gain = 320.0


def split_np(x):
    high = x.astype(jnp.bfloat16)
    low = (x - high.astype(np.float64)).astype(jnp.bfloat16)
    return high, low


def split(x):
    high = x.astype(jnp.bfloat16)
    low = (x - high.astype(jnp.float32)).astype(jnp.bfloat16)
    return high, low


@functools.lru_cache(maxsize=None)
def tables(width, rows):
    blocks = width // LANES
    half = blocks // 2 + 1
    tile = rows + 2 * HALO
    lane = np.arange(LANES)
    t = np.arange(tile)
    basis, freq = [], []
    for u in range(tile // 2 + 1):
        scale = np.sqrt((1 if u in (0, tile / 2) else 2) / tile)
        basis.append(scale * np.cos(2 * np.pi * (u * t % tile) / tile))
        freq.append(u)
        if u not in (0, tile / 2):
            basis.append(scale * np.sin(2 * np.pi * (u * t % tile) / tile))
            freq.append(u)
    basis, freq = np.stack(basis), np.array(freq)
    own = basis[:, HALO : HALO + rows]
    top, bottom = basis[:, :HALO], basis[:, HALO + rows :]
    mix = []
    for first, second in ((bottom, top), (top, bottom)):
        high, low = split_np(np.concatenate([own, first, second], axis=1))
        mix.append(np.concatenate([high, high, low], axis=1))
    mix = np.stack(mix)
    high, low = split_np(own.T)
    back = np.concatenate([high, high, low], axis=1)
    k = np.arange(half)
    phase = 2 * np.pi * (k[:, None] * lane[None, :] % width) / width
    turn = np.stack([np.cos(phase), np.sin(phase)]).astype(np.float32)
    angle = 2 * np.pi * (lane[:, None] * lane[None, :] % LANES) / LANES
    c, s = np.cos(angle), np.sin(angle)
    forward = split_np(np.block([[c, -s], [s, c]]))
    inverse = split_np(np.block([[c, s], [-s, c]]))
    v = (k[:, None] + blocks * lane[None, :]).astype(np.float64)
    folded = np.minimum(v, width - v)
    ramp = ramp_gain * (folded / width) * (0.5 + 0.5 * np.cos(2 * np.pi * folded / width))
    weight = np.where((k == 0) | (2 * k == blocks), 1.0, 2.0)[:, None] / width
    lam = 4 * np.sin(np.pi * freq / tile)[None, :, None] ** 2 + 4 * np.sin(np.pi * v / width)[:, None, :] ** 2
    filt = ((ramp * weight)[:, None, :] / (1 + paganin_beta * lam)).astype(np.float32)
    column = LANES * np.arange(blocks + 1)[:, None, None] + lane[None, None, :]
    phase = 2 * np.pi * (k[None, :, None] * column % width) / width
    pad = -half % 8
    out_phase = np.stack([np.cos(phase), -np.sin(phase)], axis=1)
    out_phase = np.pad(out_phase, ((0, 0), (0, 0), (0, pad), (0, 0))).astype(np.float32)
    return mix, back, turn, *forward, *inverse, filt, out_phase


def real_dft(x):
    n = len(x)
    h = n // 2
    plus = {a: x[a] + x[n - a] for a in range(1, h)}
    minus = {a: x[a] - x[n - a] for a in range(1, h)}
    re, im = [None] * (h + 1), [None] * (h + 1)

    def total(terms):
        acc = None
        for c, y in terms:
            if abs(c) < 1e-12:
                continue
            z = y if c == 1.0 else (-y if c == -1.0 else y * np.float32(c))
            acc = z if acc is None else acc + z
        return acc

    def cos(m):
        return float(np.round(np.cos(2 * np.pi * (m % n) / n), 15))

    def sin(m):
        return float(np.round(np.sin(2 * np.pi * (m % n) / n), 15))

    for k in range(h // 2 + 1):
        ends = {0: x[0], h: x[h]}
        even = total([(cos(a * k), ends.get(a, plus.get(a))) for a in range(0, h + 1, 2)])
        odd = total([(cos(a * k), ends.get(a, plus.get(a))) for a in range(1, h + 1, 2)])
        re[k] = even if odd is None else even + odd
        re[h - k] = even if odd is None else even - odd
        even = total([(sin(a * k), minus[a]) for a in range(2, h, 2)])
        odd = total([(sin(a * k), minus[a]) for a in range(1, h, 2)])
        parts = [y for y in (even, odd) if y is not None]
        if parts:
            im[k] = -parts[0] if len(parts) == 1 else -(even + odd)
            if h - k != k:
                im[h - k] = (even - odd) if len(parts) == 2 else (even if odd is None else -odd)
    return re, im


def chain(regions, packed, starts, own, first, second, mix, back, turn, fwd_hi, fwd_lo, inv_hi, inv_lo, filt, out_phase, *rest):
    outs, (zhi, zlo, area) = rest[:-3], rest[-3:]
    rows, width = own.shape
    blocks = width // LANES
    half = blocks // 2 + 1
    tile = rows + 2 * HALO
    dot = functools.partial(jnp.dot, preferred_element_type=jnp.float32)
    parity = lax.rem(lax.axis_index("row"), 2)
    me = lax.axis_index("ang")
    halo = jnp.concatenate([first[...].astype(jnp.float32), second[...].astype(jnp.float32)], axis=0)
    high, low = split(jnp.concatenate([own[...], halo], axis=0))
    mixed = dot(mix[parity], jnp.concatenate([high, low, high], axis=0))
    pieces = []
    for j in range(0, tile, 8):
        pieces.append(real_dft([mixed[j : j + 8, LANES * a : LANES * (a + 1)] for a in range(blocks)]))
    for k in range(half):
        re = jnp.concatenate([p[0][k] for p in pieces], axis=0)
        c, s = turn[0, k : k + 1, :], turn[1, k : k + 1, :]
        if pieces[0][1][k] is None:
            turned = jnp.concatenate([re * c, -re * s], axis=1)
        else:
            im = jnp.concatenate([p[1][k] for p in pieces], axis=0)
            turned = jnp.concatenate([re * c + im * s, im * c - re * s], axis=1)
        zhi[k * tile : (k + 1) * tile, :], zlo[k * tile : (k + 1) * tile, :] = split(turned)
    spec = dot(zhi[...], fwd_hi[...]) + dot(zlo[...], fwd_hi[...]) + dot(zhi[...], fwd_lo[...])
    for k in range(half):
        part = spec[k * tile : (k + 1) * tile]
        g = filt[k]
        zhi[k * tile : (k + 1) * tile, :], zlo[k * tile : (k + 1) * tile, :] = split(
            jnp.concatenate([part[:, :LANES] * g, part[:, LANES:] * g], axis=1)
        )
    area[...] = dot(zhi[...], inv_hi[...]) + dot(zlo[...], inv_hi[...]) + dot(zhi[...], inv_lo[...])
    lanes = lax.broadcasted_iota(jnp.int32, (1, LANES), 1)

    def region(r):
        start = starts[me, r]
        block, offset = start // LANES, lax.rem(start, LANES)
        here, after = out_phase[block], out_phase[block + 1]
        phase = jnp.where((lanes >= offset)[None], here, after)
        acc = None
        for k in range(half):
            v = area[k * tile : (k + 1) * tile, :]
            term = v[:, :LANES] * phase[0, k : k + 1, :] + v[:, LANES:] * phase[1, k : k + 1, :]
            acc = term if acc is None else acc + term
        high, low = split(acc)
        value = dot(back[...], jnp.concatenate([high, low, high], axis=0))
        return value, offset

    if packed:
        cb = packed
        for i, out in enumerate(outs):
            value, offset = region(partner(me, i, regions))
            value = pltpu.roll(value, lax.rem(me * cb + LANES - offset, LANES), 1)
            keep = (lanes >= me * cb) & (lanes < (me + 1) * cb)
            out[...] = jnp.where(keep, value, 0.0).astype(out.dtype)
    else:

        @pl.loop(0, regions)
        def _(r):
            value, offset = region(r)
            outs[0][r] = pltpu.roll(value, lax.rem(LANES - offset, LANES), 1).astype(outs[0].dtype)


def partner(me, i, count):
    return me ^ i if count & (count - 1) == 0 else lax.rem(me + i, count)


def matchings(count):
    for begin in (0, 1):
        ends = [(i, i + 1) for i in range(begin, count - 1, 2)]
        yield ends + [(j, i) for i, j in ends]


def body(projections, flats, block_start, bp_weights):
    angles_dev, rows, width = projections.shape
    cb, pixels = bp_weights.shape[1:]
    regions, row_count = lax.axis_size("ang"), lax.axis_size("row")
    contrast = 1.0 - projections[0].astype(jnp.float32) / flats
    narrow = contrast.astype(jnp.bfloat16)
    initial, last = narrow[:HALO], narrow[rows - HALO :]
    even = lax.rem(lax.axis_index("row"), 2) == 0
    sent = (jnp.where(even, last, initial), jnp.where(even, initial, last))
    halo = [lax.ppermute(x, "row", pairs) if pairs else jnp.zeros_like(x) for x, pairs in zip(sent, matchings(row_count))]
    consts = tables(width, rows)
    packed = cb if regions * cb <= LANES else 0
    tile, half = rows + 2 * HALO, width // LANES // 2 + 1
    if packed:
        shapes = [jax.ShapeDtypeStruct((rows, LANES), jnp.bfloat16)] * regions
    else:
        shapes = [jax.ShapeDtypeStruct((regions, rows, LANES), jnp.bfloat16)]
    vmem = pl.BlockSpec(memory_space=pltpu.VMEM)
    blocks = pl.pallas_call(
        functools.partial(chain, regions, packed),
        out_shape=shapes,
        in_specs=[pl.BlockSpec(memory_space=pltpu.SMEM)] + [vmem] * (3 + len(consts)),
        out_specs=[vmem] * len(shapes),
        scratch_shapes=[
            pltpu.VMEM((half * tile, 2 * LANES), jnp.bfloat16),
            pltpu.VMEM((half * tile, 2 * LANES), jnp.bfloat16),
            pltpu.VMEM((half * tile, 2 * LANES), jnp.float32),
        ],
        name="chain",
    )(block_start, contrast, *halo, *map(jnp.asarray, consts))
    if packed:
        total = blocks[0]
        for i in range(1, regions):
            pairs = [(a, int(partner(a, i, regions))) if regions & (regions - 1) == 0 else (a, (a + i) % regions) for a in range(regions)]
            total = total + lax.ppermute(blocks[i], "ang", pairs)
        weights = bp_weights.reshape(regions * cb, pixels)
        return jnp.dot(total[:, : regions * cb], weights, preferred_element_type=jnp.float32)
    mine = lax.all_to_all(blocks[0][:, :, :cb], "ang", 0, 0, tiled=True)
    return jnp.einsum("arc,acp->rp", mine, bp_weights, preferred_element_type=jnp.float32)


def solution(mesh):
    placed = (P(("scan", "ang"), "row", None), P(("scan", "row"), None), P(), P(None, None, "ang"))
    return jax.shard_map(
        body, mesh=mesh, in_specs=placed, out_specs=P(("scan", "row"), "ang"), check_vma=False
    )
```

time: 34.1 us -> 21.5 us (0.63)
  blocking collectives: 14 us -> 0 us
  matrix products: 8.87 us -> 0.73 us
  starting transfers between devices: 3.69 us -> 9.64 us
  waiting for transfers between devices: 2.63 us -> 5.87 us
  Pallas kernels: 0 us -> 2.84 us
  local copies, waits for them, and re-layouts: 2.31 us -> 0.62 us
  other arithmetic: 2.17 us -> 1.59 us
    all_gather x1 -> x0, blocking collectives: 14 us -> none  [body(): lax.all_gather(sinogram, 'ang', axis=0, tiled=True)]
    dot_general x21 -> x1, matrix products: 8.87 us -> 0.73 us  [body(): jnp.dot(total[:, :regions * cb], weights, preferred_element_type=jnp.floa...]
    ppermute x2 -> x5, starting transfers between devices: 3.69 us -> 9.64 us  [the longest x2 5.06 us: body(): lax.ppermute(x, 'row', pairs)]
    ppermute x2 -> x5, waiting for transfers between devices: 2.63 us -> 5.87 us  [the longest x3 5.03 us: body(): total = total + lax.ppermute(blocks[i], 'ang', pairs)]
    pallas_call x0 -> x1, Pallas kernels: none -> 2.84 us  [body(): pl.pallas_call(functools.partial(chain, regions, packed), out_shape=shape...]
    all_gather x1 -> x0, local copies, waits for them, and re-layouts: 1.5 us -> none  [body(): lax.all_gather(sinogram, 'ang', axis=0, tiled=True)]
    gather x1 -> x0, other arithmetic: 0.87 us -> none  [cut_block(): return lax.dynamic_slice(sheet, (0, begin), (rows_dev, cb_width))]
    gather x1 -> x0, local copies, waits for them, and re-layouts: 0.74 us -> none  [cut_block(): return lax.dynamic_slice(sheet, (0, begin), (rows_dev, cb_width))]
  transfers between devices with their start and end apart: 2 -> 5, of which waited for: 1 -> 3; matrix products, arithmetic and copies ran while one was open for 4% -> 0% of each run, Pallas kernels for 0% -> 0%
where the time goes in v1:
time: 21.5 us; the launch traced here: 21.3 us
  starting transfers between devices  9.64 us (45%)
  waiting for transfers between devices  5.87 us (27%)
  Pallas kernels  2.84 us (13%)
  other arithmetic  1.59 us (7%)
  matrix products  0.73 us (3%)
  local copies, waits for them, and re-layouts  0.62 us (3%)
    ppermute x2, starting transfers between devices, body(): lax.ppermute(x, 'row', pairs)  5.06 us
    ppermute x3, waiting for transfers between devices, body(): total = total + lax.ppermute(blocks[i], 'ang', pairs)  5.03 us
    ppermute x3, starting transfers between devices, body(): total = total + lax.ppermute(blocks[i], 'ang', pairs)  4.59 us
    pallas_call x1, Pallas kernels, body(): pl.pallas_call(functools.partial(chain, regions, packed), out_shape=shape...  2.84 us
    convert_element_type x1, other arithmetic, body(): narrow = contrast.astype(jnp.bfloat16)  1.56 us
    ppermute x2, waiting for transfers between devices, body(): lax.ppermute(x, 'row', pairs)  0.84 us
    dot_general x1, matrix products, body(): jnp.dot(total[:, :regions * cb], weights, preferred_element_type=jnp.floa...  0.73 us
    unnamed x12, local copies, waits for them, and re-layouts  0.62 us
  transfers between devices with their start and end apart: 5, of which 3 were waited for; matrix products, arithmetic and copies ran while one was open for 0% of the time, Pallas kernels for 0%

profile of v1, /device:TPU:0, one launch (start us, length us, event | category | flops | bytes accessed | tf_op | source)
XLA Modules:
  0.0 21.3 jit_solution(11132018349550202012)
XLA Ops:
  0.0 0.0 copy-start
  0.0 1.6 %fusion.5 = (bf16[8,2560]{1,0:T(8,128)(2,1)S(1)}, f32[8,2560]{1,0:T(8,128)}) fusion(f32[8,2560]{1,0:T(8,128)} %param.14, bf16[1,8,2560]{2,1,0:T(8,128)(2,1)} %param.13), kind=kLoop, calls=%fused_computation.8 | loop fusion | flops 81920 | bytes 245760 | tf_op jit(solution)/shard_map/convert_element_type | solution.py:191
  1.6 0.7 %collective-permute-start.1 = (bf16[4,2560]{1,0:T(4,128)(2,1)S(1)}, bf16[4,2560]{1,0:T(4,128)(2,1)S(1)}, u32[]{:S(2)}, u32[]{:S(2)}) collective-permute-start(bf16[4,2560]{1,0:T(4,128)(2,1)S(1)} %get-tuple-element.15), channel_id=1, source_target_pairs={{1,2},{2,1},{5,6},{6,5},{9,10},{10,9},{13,14},{14,13},{17,18},{18,... | collective-permute-start | bytes 61448 | tf_op jit(solution)/shard_map/ppermute | solution.py:195
  2.3 4.4 %collective-permute-start = (bf16[4,2560]{1,0:T(4,128)(2,1)S(1)}, bf16[4,2560]{1,0:T(4,128)(2,1)S(1)}, u32[]{:S(2)}, u32[]{:S(2)}) collective-permute-start(bf16[4,2560]{1,0:T(4,128)(2,1)S(1)} %get-tuple-element.16), channel_id=1, source_target_pairs={{0,1},{2,3},{1,0},{3,2},{4,5},{6,7},{5,4},{7,6},{8,9},{10,11},{9,8... | collective-permute-start | bytes 61448 | tf_op jit(solution)/shard_map/ppermute | solution.py:195
  6.7 0.0 collective-permute-done.1.second
  6.7 0.0 copy-start.1
  6.7 0.8 %collective-permute-done.first = bf16[4,2560]{1,0:T(4,128)(2,1)S(1)} collective-permute-done((bf16[4,2560]{1,0:T(4,128)(2,1)S(1)}, bf16[4,2560]{1,0:T(4,128)(2,1)S(1)}, u32[]{:S(2)}, u32[]{:S(2)}) %collective-permute-start) | collective-permute-done | bytes 20512 | tf_op jit(solution)/shard_map/ppermute | solution.py:195
  7.5 0.0 copy-start.2
  7.5 0.0 copy-done.1
  7.5 0.6 %copy-done.2 = bf16[4,2560]{1,0:T(4,128)(2,1)} copy-done((bf16[4,2560]{1,0:T(4,128)(2,1)}, bf16[4,2560]{1,0:T(4,128)(2,1)S(1)}, u32[]{:S(2)}) %copy-start.2) | copy-done | bytes 20504
  8.1 2.8 %chain.1 = (bf16[8,128]{1,0:T(8,128)(2,1)}, bf16[8,128]{1,0:T(8,128)(2,1)}, bf16[8,128]{1,0:T(8,128)(2,1)}, bf16[8,128]{1,0:T(8,128)(2,1)}) custom-call(s32[4,4]{1,0:T(4,128)} %starts.1, f32[8,2560]{1,0:T(8,128)} %get-tuple-element.14.own, bf16[4,2560]{1,0:T(4,128)(2,1)} %copy-done.2, bf16[4,2560]{1,0:T(4,128)(2,1)} %copy-done.1, ...), custom_call_target="tpu_custom_call" | custom-call | tf_op jit(solution)/shard_map/chain/pallas_call | solution.py:204
  11.0 0.0 copy-start.5
  11.0 0.0 copy-start.4
  11.0 1.6 %collective-permute-start.2 = (bf16[8,128]{1,0:T(8,128)(2,1)}, bf16[8,128]{1,0:T(8,128)(2,1)S(1)}, u32[]{:S(2)}, u32[]{:S(2)}) collective-permute-start(bf16[8,128]{1,0:T(8,128)(2,1)} %get-tuple-element.10), channel_id=1, source_target_pairs={{0,4},{4,0},{8,12},{12,8},{1,5},{5,1},{9,13},{13,9},{2,6},{6,2},{1... | collective-permute-start | bytes 6152 | tf_op jit(solution)/shard_map/ppermute | solution.py:220
  12.6 0.0 copy-done.5
  12.6 2.6 %collective-permute-start.3 = (bf16[8,128]{1,0:T(8,128)(2,1)S(1)}, bf16[8,128]{1,0:T(8,128)(2,1)S(1)}, u32[]{:S(2)}, u32[]{:S(2)}) collective-permute-start(bf16[8,128]{1,0:T(8,128)(2,1)S(1)} %copy-done.5), channel_id=1, source_target_pairs={{0,8},{4,12},{8,0},{12,4},{1,9},{5,13},{9,1},{13,5},{2,10},{6,14},... | collective-permute-start | bytes 6152 | tf_op jit(solution)/shard_map/ppermute | solution.py:220
  15.2 0.0 copy-done.4
  15.2 0.0 copy-start.3
  15.2 0.4 %collective-permute-start.4 = (bf16[8,128]{1,0:T(8,128)(2,1)S(1)}, bf16[8,128]{1,0:T(8,128)(2,1)S(1)}, u32[]{:S(2)}, u32[]{:S(2)}) collective-permute-start(bf16[8,128]{1,0:T(8,128)(2,1)S(1)} %copy-done.4), channel_id=1, source_target_pairs={{0,12},{4,8},{8,4},{12,0},{1,13},{5,9},{9,5},{13,1},{2,14},{6,10},... | collective-permute-start | bytes 6152 | tf_op jit(solution)/shard_map/ppermute | solution.py:220
  15.6 0.0 collective-permute-done.2
  15.6 1.5 %collective-permute-done.3 = bf16[8,128]{1,0:T(8,128)(2,1)S(1)} collective-permute-done((bf16[8,128]{1,0:T(8,128)(2,1)S(1)}, bf16[8,128]{1,0:T(8,128)(2,1)S(1)}, u32[]{:S(2)}, u32[]{:S(2)}) %collective-permute-start.3) | collective-permute-done | bytes 2080 | tf_op jit(solution)/shard_map/ppermute | solution.py:220
  17.1 3.5 %collective-permute-done.4 = bf16[8,128]{1,0:T(8,128)(2,1)S(1)} collective-permute-done((bf16[8,128]{1,0:T(8,128)(2,1)S(1)}, bf16[8,128]{1,0:T(8,128)(2,1)S(1)}, u32[]{:S(2)}, u32[]{:S(2)}) %collective-permute-start.4) | collective-permute-done | bytes 2080 | tf_op jit(solution)/shard_map/ppermute | solution.py:220
  20.6 0.0 copy-done
  20.6 0.0 copy-done.3
  20.6 0.7 %fusion.1 = f32[8,256]{1,0:T(8,128)} fusion(bf16[128,256]{1,0:T(8,128)(2,1)S(1)} %bitcast.6, bf16[8,128]{1,0:T(8,128)(2,1)S(1)} %collective-permute-done.4, bf16[8,128]{1,0:T(8,128)(2,1)S(1)} %collective-permute-done.3, bf16[8,128]{1,0:T(8,128)(2,1)S(1)} %copy-done.3, bf16[8,128]{1,0:T(8,128)(2,1)S(1)} %collective-permute-done.2), kind=kOutput, calls=%fused_computation.4 | convolution fusion | flops 527360 | bytes 81920 | tf_op jit(solution)/shard_map/dot_general | solution.py:222
  (1 shorter events, 0.0 us)
Async XLA Ops:
  0.0 20.6 %copy-start = (bf16[4,32,256]{2,1,0:T(8,128)(2,1)S(1)}, bf16[4,32,256]{2,1,0:T(8,128)(2,1)}, u32[]{:S(2)}) copy-start(bf16[4,32,256]{2,1,0:T(8,128)(2,1)} %param.16) | copy-start | bytes 196612
  1.6 5.1 %collective-permute-start.1 = (bf16[4,2560]{1,0:T(4,128)(2,1)S(1)}, bf16[4,2560]{1,0:T(4,128)(2,1)S(1)}, u32[]{:S(2)}, u32[]{:S(2)}) collective-permute-start(bf16[4,2560]{1,0:T(4,128)(2,1)S(1)} %get-tuple-element.15), channel_id=1, source_target_pairs={{1,2},{2,1},{5,6},{6,5},{9,10},{10,9},{13,14},{14,13},{17,18},{18,... | collective-permute-start | bytes 61448 | tf_op jit(solution)/shard_map/ppermute | solution.py:195
  2.3 5.2 %collective-permute-start = (bf16[4,2560]{1,0:T(4,128)(2,1)S(1)}, bf16[4,2560]{1,0:T(4,128)(2,1)S(1)}, u32[]{:S(2)}, u32[]{:S(2)}) collective-permute-start(bf16[4,2560]{1,0:T(4,128)(2,1)S(1)} %get-tuple-element.16), channel_id=1, source_target_pairs={{0,1},{2,3},{1,0},{3,2},{4,5},{6,7},{5,4},{7,6},{8,9},{10,11},{9,8... | collective-permute-start | bytes 61448 | tf_op jit(solution)/shard_map/ppermute | solution.py:195
  6.7 0.8 %copy-start.1 = (bf16[4,2560]{1,0:T(4,128)(2,1)}, bf16[4,2560]{1,0:T(4,128)(2,1)S(1)}, u32[]{:S(2)}) copy-start(bf16[4,2560]{1,0:T(4,128)(2,1)S(1)} %collective-permute-done.1.second) | copy-start | bytes 61444
  7.5 0.6 %copy-start.2 = (bf16[4,2560]{1,0:T(4,128)(2,1)}, bf16[4,2560]{1,0:T(4,128)(2,1)S(1)}, u32[]{:S(2)}) copy-start(bf16[4,2560]{1,0:T(4,128)(2,1)S(1)} %collective-permute-done.first) | copy-start | bytes 61444
  11.0 1.7 %copy-start.5 = (bf16[8,128]{1,0:T(8,128)(2,1)S(1)}, bf16[8,128]{1,0:T(8,128)(2,1)}, u32[]{:S(2)}) copy-start(bf16[8,128]{1,0:T(8,128)(2,1)} %get-tuple-element.11) | copy-start | bytes 6148
  11.0 4.2 %copy-start.4 = (bf16[8,128]{1,0:T(8,128)(2,1)S(1)}, bf16[8,128]{1,0:T(8,128)(2,1)}, u32[]{:S(2)}) copy-start(bf16[8,128]{1,0:T(8,128)(2,1)} %get-tuple-element.12) | copy-start | bytes 6148
  11.0 4.6 %collective-permute-start.2 = (bf16[8,128]{1,0:T(8,128)(2,1)}, bf16[8,128]{1,0:T(8,128)(2,1)S(1)}, u32[]{:S(2)}, u32[]{:S(2)}) collective-permute-start(bf16[8,128]{1,0:T(8,128)(2,1)} %get-tuple-element.10), channel_id=1, source_target_pairs={{0,4},{4,0},{8,12},{12,8},{1,5},{5,1},{9,13},{13,9},{2,6},{6,2},{1... | collective-permute-start | bytes 6152 | tf_op jit(solution)/shard_map/ppermute | solution.py:220
  12.6 4.5 %collective-permute-start.3 = (bf16[8,128]{1,0:T(8,128)(2,1)S(1)}, bf16[8,128]{1,0:T(8,128)(2,1)S(1)}, u32[]{:S(2)}, u32[]{:S(2)}) collective-permute-start(bf16[8,128]{1,0:T(8,128)(2,1)S(1)} %copy-done.5), channel_id=1, source_target_pairs={{0,8},{4,12},{8,0},{12,4},{1,9},{5,13},{9,1},{13,5},{2,10},{6,14},... | collective-permute-start | bytes 6152 | tf_op jit(solution)/shard_map/ppermute | solution.py:220
  15.2 5.4 %copy-start.3 = (bf16[8,128]{1,0:T(8,128)(2,1)S(1)}, bf16[8,128]{1,0:T(8,128)(2,1)}, u32[]{:S(2)}) copy-start(bf16[8,128]{1,0:T(8,128)(2,1)} %get-tuple-element.9) | copy-start | bytes 6148
  15.2 5.4 %collective-permute-start.4 = (bf16[8,128]{1,0:T(8,128)(2,1)S(1)}, bf16[8,128]{1,0:T(8,128)(2,1)S(1)}, u32[]{:S(2)}, u32[]{:S(2)}) collective-permute-start(bf16[8,128]{1,0:T(8,128)(2,1)S(1)} %copy-done.4), channel_id=1, source_target_pairs={{0,12},{4,8},{8,4},{12,0},{1,13},{5,9},{9,5},{13,1},{2,14},{6,10},... | collective-permute-start | bytes 6152 | tf_op jit(solution)/shard_map/ppermute | solution.py:220

commit v2 on v1

v2 whole, which is shorter than its diff:
```python
import functools

import jax
import jax.numpy as jnp
import numpy as np
from jax import lax
from jax.experimental import pallas as pl
from jax.experimental.pallas import tpu as pltpu
from jax.sharding import PartitionSpec as P

HALO = 4
LANES = 128
paganin_beta = 8.0
ramp_gain = 320.0


def split_np(x):
    high = x.astype(jnp.bfloat16)
    low = (x - high.astype(np.float64)).astype(jnp.bfloat16)
    return high, low


def split(x):
    high = x.astype(jnp.bfloat16)
    low = (x - high.astype(jnp.float32)).astype(jnp.bfloat16)
    return high, low


@functools.lru_cache(maxsize=None)
def tables(width, rows):
    blocks = width // LANES
    half = blocks // 2 + 1
    depth = half + -half % 8
    tile = rows + 2 * HALO
    lane = np.arange(LANES)
    t = np.arange(tile)
    basis, freq = [], []
    for u in range(tile // 2 + 1):
        scale = np.sqrt((1 if u in (0, tile / 2) else 2) / tile)
        basis.append(scale * np.cos(2 * np.pi * (u * t % tile) / tile))
        freq.append(u)
        if u not in (0, tile / 2):
            basis.append(scale * np.sin(2 * np.pi * (u * t % tile) / tile))
            freq.append(u)
    basis, freq = np.stack(basis), np.array(freq)
    own = basis[:, HALO : HALO + rows]
    top, bottom = basis[:, :HALO], basis[:, HALO + rows :]
    high, low = split_np(own)
    mix = [np.concatenate([high, high, low], axis=1)]
    for first, second in ((bottom, top), (top, bottom)):
        mix.append(np.concatenate(split_np(np.concatenate([first, second], axis=1)), axis=1))
    high, low = split_np(own.T)
    back = np.concatenate([high, high, low], axis=1)
    k = np.arange(half)
    phase = 2 * np.pi * (k[:, None] * lane[None, :] % width) / width
    turn = [np.pad(x, ((0, depth - half), (0, 0))) for x in (np.cos(phase), np.sin(phase))]
    angle = 2 * np.pi * (lane[:, None] * lane[None, :] % LANES) / LANES
    c, s = np.cos(angle), np.sin(angle)
    forward = split_np(np.block([[c, -s], [s, c]]))
    v = (k[:, None] + blocks * lane[None, :]).astype(np.float64)
    folded = np.minimum(v, width - v)
    ramp = ramp_gain * (folded / width) * (0.5 + 0.5 * np.cos(2 * np.pi * folded / width))
    weight = np.where((k == 0) | (2 * k == blocks), 1.0, 2.0)[:, None] / width
    across = 4 * np.sin(np.pi * v / width) ** 2
    along = 4 * np.sin(np.pi * freq / tile)[:, None] ** 2
    parts = [np.pad(x, ((0, depth - half), (0, 0))) for x in (ramp * weight, 1 + paganin_beta * across)]
    parts += [np.broadcast_to(paganin_beta * along, (tile, LANES))]
    phase = 2 * np.pi * (k[:, None] * lane[None, :] % blocks) / blocks
    jump = [np.pad(x, ((0, depth - half), (0, 0))) for x in (np.cos(phase), np.sin(phase))]
    paired = np.concatenate(split_np(np.concatenate([*turn, *jump, *parts])), axis=1)
    parts = [*forward, paired, *mix, back]
    return np.concatenate([np.pad(x, ((0, -x.shape[0] % 16), (0, 2 * LANES - x.shape[1]))) for x in parts])


def layout(width, rows):
    blocks, half, depth, tile = sizes(width, rows)
    turn = 4 * LANES
    gain = turn + 4 * depth
    mix = gain + 2 * depth + tile
    return dict(turn=turn, jump=turn + 2 * depth, gain=gain, mix=mix, back=mix + 3 * tile)


def wide(table, begin, count):
    x = table[begin : begin + count, :].astype(jnp.float32)
    return x[:, :LANES] + x[:, LANES:]


def real_dft(x):
    n = len(x)
    h = n // 2
    plus = {a: x[a] + x[n - a] for a in range(1, h)}
    minus = {a: x[a] - x[n - a] for a in range(1, h)}
    re, im = [None] * (h + 1), [None] * (h + 1)

    def total(terms):
        acc = None
        for c, y in terms:
            if abs(c) < 1e-12:
                continue
            z = y if c == 1.0 else (-y if c == -1.0 else y * np.float32(c))
            acc = z if acc is None else acc + z
        return acc

    def cos(m):
        return float(np.round(np.cos(2 * np.pi * (m % n) / n), 15))

    def sin(m):
        return float(np.round(np.sin(2 * np.pi * (m % n) / n), 15))

    for k in range(h // 2 + 1):
        ends = {0: x[0], h: x[h]}
        even = total([(cos(a * k), ends.get(a, plus.get(a))) for a in range(0, h + 1, 2)])
        odd = total([(cos(a * k), ends.get(a, plus.get(a))) for a in range(1, h + 1, 2)])
        re[k] = even if odd is None else even + odd
        re[h - k] = even if odd is None else even - odd
        even = total([(sin(a * k), minus[a]) for a in range(2, h, 2)])
        odd = total([(sin(a * k), minus[a]) for a in range(1, h, 2)])
        parts = [y for y in (even, odd) if y is not None]
        if parts:
            im[k] = -parts[0] if len(parts) == 1 else -(even + odd)
            if h - k != k:
                im[h - k] = (even - odd) if len(parts) == 2 else (even if odd is None else -odd)
    return re, im


def sizes(width, rows):
    blocks = width // LANES
    half = blocks // 2 + 1
    return blocks, half, half + -half % 8, rows + 2 * HALO


dot = functools.partial(jnp.dot, preferred_element_type=jnp.float32)


def spectrum(mixed, table, zhi, zlo):
    tile, width = mixed.shape
    blocks, half, depth, _ = sizes(width, tile - 2 * HALO)
    turn = wide(table, layout(width, tile - 2 * HALO)["turn"], 2 * depth)
    pieces = []
    for j in range(0, tile, 8):
        pieces.append(real_dft([mixed[j : j + 8, LANES * a : LANES * (a + 1)] for a in range(blocks)]))
    for k in range(half):
        re = jnp.concatenate([p[0][k] for p in pieces], axis=0)
        c, s = turn[k : k + 1], turn[depth + k : depth + k + 1]
        if pieces[0][1][k] is None:
            turned = jnp.concatenate([re * c, -re * s], axis=1)
        else:
            im = jnp.concatenate([p[1][k] for p in pieces], axis=0)
            turned = jnp.concatenate([re * c + im * s, im * c - re * s], axis=1)
        zhi[k * tile : (k + 1) * tile, :], zlo[k * tile : (k + 1) * tile, :] = split(turned)
    n = 2 * LANES
    high, low = table[:n, :], table[n : 2 * n, :]
    return dot(zhi[...], high) + dot(zlo[...], high) + dot(zhi[...], low)


def prepare(regions, cb, starts, own, table, spec, filt, phases, shifts, zhi, zlo):
    rows, width = own.shape
    blocks, half, depth, tile = sizes(width, rows)
    at = layout(width, rows)
    me = lax.axis_index("ang")
    high, low = split(own[...])
    mix = table[at["mix"] : at["mix"] + tile, : 3 * rows]
    spec[...] = spectrum(dot(mix, jnp.concatenate([high, low, high], axis=0)), table, zhi, zlo)
    gain = wide(table, at["gain"], 2 * depth + tile)
    for k in range(half):
        lam = gain[2 * depth :] + gain[depth + k : depth + k + 1]
        filt[k * tile : (k + 1) * tile, :] = gain[k : k + 1] / lam
    lanes = lax.broadcasted_iota(jnp.int32, (1, LANES), 1)
    shifts[...] = jnp.zeros_like(shifts)
    turn, jump = wide(table, at["turn"], 2 * depth), wide(table, at["jump"], 2 * depth)

    def region(i):
        start = starts[me, partner(me, i, regions) if cb else i]
        block, offset = start // LANES, lax.rem(start, LANES)
        shifts[...] += jnp.where(lanes == i, lax.rem(me * cb + LANES - offset, LANES), 0).astype(jnp.float32)
        picked = []
        for b in (block, block + 1):
            picked.append(jnp.sum(jnp.where(lanes == b, jump, 0.0), axis=1, keepdims=True))
        far = jnp.where(lanes >= offset, picked[0], picked[1])
        c, s, fc, fs = turn[:depth], turn[depth:], far[:depth], far[depth:]
        phases[i] = jnp.concatenate([c * fc - s * fs, -(s * fc + c * fs)], axis=0)

    if cb:
        for i in range(regions):
            region(i)
    else:
        pl.loop(0, regions)(region)


def chain(regions, cb, first, second, table, spec, filt, phases, shifts, *rest):
    outs, (zhi, zlo, area) = rest[:-3], rest[-3:]
    width, rows = first.shape[1], outs[0].shape[-2]
    blocks, half, depth, tile = sizes(width, rows)
    where = layout(width, rows)
    n = 2 * LANES
    parity = lax.rem(lax.axis_index("row"), 2)
    halo = jnp.concatenate([first[...].astype(jnp.float32), second[...].astype(jnp.float32)], axis=0)
    halo = jnp.concatenate([halo, halo], axis=0).astype(jnp.bfloat16)
    mix = table[pl.ds(where["mix"] + pl.multiple_of((1 + parity) * tile, tile), tile), : 4 * HALO]
    whole = spectrum(dot(mix, halo), table, zhi, zlo)
    for k in range(half):
        at = slice(k * tile, (k + 1) * tile)
        part = whole[at] + spec[at, :]
        g = filt[at, :]
        zhi[at, :], zlo[at, :] = split(jnp.concatenate([part[:, :LANES] * g, part[:, LANES:] * g], axis=1))
    turned = functools.partial(lax.dot_general, dimension_numbers=(((1,), (1,)), ((), ())), preferred_element_type=jnp.float32)
    high, low = table[:n, :], table[n : 2 * n, :]
    area[...] = turned(zhi[...], high) + turned(zlo[...], high) + turned(zhi[...], low)
    lanes = lax.broadcasted_iota(jnp.int32, (1, LANES), 1)
    back = table[where["back"] : where["back"] + rows, : 3 * tile]

    def region(i):
        phase = phases[i]
        acc = None
        for k in range(half):
            v = area[k * tile : (k + 1) * tile, :]
            term = v[:, :LANES] * phase[k : k + 1] + v[:, LANES:] * phase[depth + k : depth + k + 1]
            acc = term if acc is None else acc + term
        high, low = split(acc)
        value = dot(back, jnp.concatenate([high, low, high], axis=0))
        return pltpu.roll(value, jnp.sum(jnp.where(lanes == i, shifts[...], 0.0)).astype(jnp.int32), 1)

    if cb:
        me = lax.axis_index("ang")
        keep = (lanes >= me * cb) & (lanes < (me + 1) * cb)
        for i, out in enumerate(outs):
            out[...] = jnp.where(keep, region(i), 0.0).astype(out.dtype)
    else:

        @pl.loop(0, regions)
        def _(r):
            outs[0][r] = region(r).astype(outs[0].dtype)


def partner(me, i, count):
    return me ^ i if count & (count - 1) == 0 else lax.rem(me + i, count)


def matchings(count):
    for begin in (0, 1):
        ends = [(i, i + 1) for i in range(begin, count - 1, 2)]
        yield ends + [(j, i) for i, j in ends]


def body(projections, flats, block_start, bp_weights):
    angles_dev, rows, width = projections.shape
    cb, pixels = bp_weights.shape[1:]
    regions, row_count = lax.axis_size("ang"), lax.axis_size("row")
    contrast = 1.0 - projections[0].astype(jnp.float32) / flats
    narrow = contrast.astype(jnp.bfloat16)
    initial, last = narrow[:HALO], narrow[rows - HALO :]
    even = lax.rem(lax.axis_index("row"), 2) == 0
    sent = (jnp.where(even, last, initial), jnp.where(even, initial, last))
    halo = []
    for name, x, pairs in zip(("hop_a", "hop_b"), sent, matchings(row_count)):
        with jax.named_scope(name):
            halo.append(lax.ppermute(x, "row", pairs) if pairs else jnp.zeros_like(x))
    table = jnp.asarray(tables(width, rows))
    packed = cb if regions * cb <= LANES else 0
    blocks, half, depth, tile = sizes(width, rows)
    vmem = pl.BlockSpec(memory_space=pltpu.VMEM)
    halves = [pltpu.VMEM((half * tile, 2 * LANES), jnp.bfloat16)] * 2
    limit = pltpu.CompilerParams(vmem_limit_bytes=8 * 1024 * 1024)
    ready = pl.pallas_call(
        functools.partial(prepare, regions, packed),
        out_shape=[
            jax.ShapeDtypeStruct((half * tile, 2 * LANES), jnp.float32),
            jax.ShapeDtypeStruct((half * tile, LANES), jnp.float32),
            jax.ShapeDtypeStruct((regions, 2 * depth, LANES), jnp.float32),
            jax.ShapeDtypeStruct((1, LANES), jnp.float32),
        ],
        in_specs=[pl.BlockSpec(memory_space=pltpu.SMEM), vmem, vmem],
        out_specs=[vmem] * 4,
        scratch_shapes=halves,
        compiler_params=limit,
        cost_estimate=pl.CostEstimate(flops=400_000_000, bytes_accessed=2_000_000, transcendentals=0),
        name="prepare",
    )(block_start, contrast, table)
    if packed:
        shapes = [jax.ShapeDtypeStruct((rows, LANES), jnp.bfloat16)] * regions
    else:
        shapes = [jax.ShapeDtypeStruct((regions, rows, LANES), jnp.bfloat16)]
    cut = pl.pallas_call(
        functools.partial(chain, regions, packed),
        out_shape=shapes,
        in_specs=[vmem] * 7,
        out_specs=[vmem] * len(shapes),
        scratch_shapes=halves + [pltpu.VMEM((half * tile, 2 * LANES), jnp.float32)],
        compiler_params=limit,
        name="chain",
    )(*halo, table, *ready)
    if packed:
        total = cut[0]
        for i in reversed(range(1, regions)):
            pairs = [(a, int(partner(a, i, regions)) if regions & (regions - 1) == 0 else (a + i) % regions) for a in range(regions)]
            with jax.named_scope(f"ang_{i}"):
                total = total + lax.ppermute(cut[i], "ang", pairs)
        weights = bp_weights.reshape(regions * cb, pixels)
        return jnp.dot(total[:, : regions * cb], weights, preferred_element_type=jnp.float32)
    mine = lax.all_to_all(cut[0][:, :, :cb], "ang", 0, 0, tiled=True)
    return jnp.einsum("arc,acp->rp", mine, bp_weights, preferred_element_type=jnp.float32)


def solution(mesh):
    placed = (P(("scan", "ang"), "row", None), P(("scan", "row"), None), P(), P(None, None, "ang"))
    return jax.shard_map(
        body, mesh=mesh, in_specs=placed, out_specs=P(("scan", "row"), "ang"), check_vma=False
    )
```

time: 21.5 us -> 17 us (0.79)
  waiting for transfers between devices: 5.87 us -> 3.7 us
  Pallas kernels: 2.84 us -> 1.88 us
  local copies, waits for them, and re-layouts: 0.62 us -> 0.01 us
  other arithmetic: 1.59 us -> 1 us
    ppermute x5, waiting for transfers between devices: 5.87 us -> 3.7 us  [the longest x3 3.7 us: body(): total = total + lax.ppermute(cut[i], 'ang', pairs)]
    pallas_call x1, Pallas kernels: 2.84 us -> 0.92 us  [body(): pl.pallas_call(functools.partial(chain, regions, packed), out_shape=shape...]
    pallas_call x0 -> x1, Pallas kernels: none -> 0.96 us  [body(): pl.pallas_call(functools.partial(prepare, regions, packed), out_shape=[ja...]
    unnamed x12 -> x6, local copies, waits for them, and re-layouts: 0.62 us -> 0.01 us
    convert_element_type x1, other arithmetic: 1.56 us -> 0.96 us  [body(): narrow = contrast.astype(jnp.bfloat16)]
  transfers between devices with their start and end apart: 5 -> 5, of which waited for: 3 -> 2; matrix products, arithmetic and copies ran while one was open for 0% -> 0% of each run, Pallas kernels for 0% -> 6%
where the time goes in v2:
time: 17 us; the launch traced here: 16.9 us
  starting transfers between devices  9.48 us (56%)
  waiting for transfers between devices  3.7 us (22%)
  Pallas kernels  1.88 us (11%)
  other arithmetic  1 us (6%)
  matrix products  0.73 us (4%)
    ppermute x2, starting transfers between devices, body(): halo.append(lax.ppermute(x, 'row', pairs) if pairs else jnp.zeros_like(x))  5.06 us
    ppermute x3, starting transfers between devices, body(): total = total + lax.ppermute(cut[i], 'ang', pairs)  4.42 us
    ppermute x3, waiting for transfers between devices, body(): total = total + lax.ppermute(cut[i], 'ang', pairs)  3.7 us
    pallas_call x1, Pallas kernels, body(): pl.pallas_call(functools.partial(prepare, regions, packed), out_shape=[ja...  0.96 us
    convert_element_type x1, other arithmetic, body(): narrow = contrast.astype(jnp.bfloat16)  0.96 us
    pallas_call x1, Pallas kernels, body(): pl.pallas_call(functools.partial(chain, regions, packed), out_shape=shape...  0.92 us
    dot_general x1, matrix products, body(): jnp.dot(total[:, :regions * cb], weights, preferred_element_type=jnp.floa...  0.73 us
  transfers between devices with their start and end apart: 5, of which 2 were waited for; matrix products, arithmetic and copies ran while one was open for 0% of the time, Pallas kernels for 6%

profile of v2, /device:TPU:0, one launch (start us, length us, event | category | flops | bytes accessed | tf_op | source)
XLA Modules:
  0.0 16.9 jit_solution(3396459704838575603)
XLA Ops:
  0.0 0.0 copy-start
  0.0 0.0 copy-start.1
  0.0 1.0 %fusion.5 = (bf16[8,2560]{1,0:T(8,128)(2,1)S(1)}, f32[8,2560]{1,0:T(8,128)S(1)}) fusion(f32[8,2560]{1,0:T(8,128)} %param.6, bf16[1,8,2560]{2,1,0:T(8,128)(2,1)} %param.5), kind=kLoop, calls=%fused_computation.8 | loop fusion | flops 81920 | bytes 245760 | tf_op jit(solution)/shard_map/convert_element_type | solution.py:250
  1.0 0.0 copy-start.2
  1.0 0.7 %collective-permute-start.1 = (bf16[4,2560]{1,0:T(4,128)(2,1)S(1)}, bf16[4,2560]{1,0:T(4,128)(2,1)S(1)}, u32[]{:S(2)}, u32[]{:S(2)}) collective-permute-start(bf16[4,2560]{1,0:T(4,128)(2,1)S(1)} %get-tuple-element.23), channel_id=1, source_target_pairs={{1,2},{2,1},{5,6},{6,5},{9,10},{10,9},{13,14},{14,13},{17,18},{18,... | collective-permute-start | bytes 61448 | tf_op jit(solution)/shard_map/hop_b/ppermute | solution.py:257
  1.7 4.4 %collective-permute-start = (bf16[4,2560]{1,0:T(4,128)(2,1)S(1)}, bf16[4,2560]{1,0:T(4,128)(2,1)S(1)}, u32[]{:S(2)}, u32[]{:S(2)}) collective-permute-start(bf16[4,2560]{1,0:T(4,128)(2,1)S(1)} %get-tuple-element.24), channel_id=1, source_target_pairs={{0,1},{2,3},{1,0},{3,2},{4,5},{6,7},{5,4},{7,6},{8,9},{10,11},{9,8... | collective-permute-start | bytes 61448 | tf_op jit(solution)/shard_map/hop_a/ppermute | solution.py:257
  6.1 0.0 copy-done.1
  6.1 0.0 copy-done.2
  6.1 1.0 %prepare.1 = (f32[176,256]{1,0:T(8,128)S(1)}, f32[176,128]{1,0:T(8,128)S(1)}, f32[4,32,128]{2,1,0:T(8,128)S(1)}, f32[1,128]{1,0:T(1,128)S(1)}) custom-call(s32[4,4]{1,0:T(4,128)S(1)} %copy-done.2, f32[8,2560]{1,0:T(8,128)S(1)} %get-tuple-element.22.own, bf16[688,256]{1,0:T(8,128)(2,1)S(1)} %copy-done.1), custom_call_target="tpu_custom_call" | custom-call | flops 400000000 | bytes 2000000 | tf_op jit(solution)/shard_map/prepare/pallas_call | solution.py:264
  7.1 0.0 collective-permute-done.1.second
  7.1 0.0 collective-permute-done.first
  7.1 0.9 %chain.1 = (bf16[8,128]{1,0:T(8,128)(2,1)S(1)}, bf16[8,128]{1,0:T(8,128)(2,1)S(1)}, bf16[8,128]{1,0:T(8,128)(2,1)S(1)}, bf16[8,128]{1,0:T(8,128)(2,1)S(1)}) custom-call(bf16[4,2560]{1,0:T(4,128)(2,1)S(1)} %collective-permute-done.first, bf16[4,2560]{1,0:T(4,128)(2,1)S(1)} %collective-permute-done.1.second, bf16[688,256]{1,0:T(8,128)(2,1)S(1)} %copy-done.1, ...), custom_call_target="tpu_custom_call" | custom-call | tf_op jit(solution)/shard_map/chain/pallas_call | solution.py:283
  8.0 3.6 %collective-permute-start.2 = (bf16[8,128]{1,0:T(8,128)(2,1)S(1)}, bf16[8,128]{1,0:T(8,128)(2,1)S(1)}, u32[]{:S(2)}, u32[]{:S(2)}) collective-permute-start(bf16[8,128]{1,0:T(8,128)(2,1)S(1)} %get-tuple-element.18), channel_id=1, source_target_pairs={{0,12},{4,8},{8,4},{12,0},{1,13},{5,9},{9,5},{13,1},{2,14},{6,10},... | collective-permute-start | bytes 6152 | tf_op jit(solution)/shard_map/ang_3/ppermute | solution.py:297
  11.6 0.0 collective-permute-start.3
  11.6 0.8 %collective-permute-start.4 = (bf16[8,128]{1,0:T(8,128)(2,1)S(1)}, bf16[8,128]{1,0:T(8,128)(2,1)S(1)}, u32[]{:S(2)}, u32[]{:S(2)}) collective-permute-start(bf16[8,128]{1,0:T(8,128)(2,1)S(1)} %get-tuple-element.20), channel_id=1, source_target_pairs={{0,4},{4,0},{8,12},{12,8},{1,5},{5,1},{9,13},{13,9},{2,6},{6,2},{1... | collective-permute-start | bytes 6152 | tf_op jit(solution)/shard_map/ang_1/ppermute | solution.py:297
  12.4 1.0 %collective-permute-done.2 = bf16[8,128]{1,0:T(8,128)(2,1)S(1)} collective-permute-done((bf16[8,128]{1,0:T(8,128)(2,1)S(1)}, bf16[8,128]{1,0:T(8,128)(2,1)S(1)}, u32[]{:S(2)}, u32[]{:S(2)}) %collective-permute-start.2) | collective-permute-done | bytes 2080 | tf_op jit(solution)/shard_map/ang_3/ppermute | solution.py:297
  13.4 2.7 %collective-permute-done.3 = bf16[8,128]{1,0:T(8,128)(2,1)S(1)} collective-permute-done((bf16[8,128]{1,0:T(8,128)(2,1)S(1)}, bf16[8,128]{1,0:T(8,128)(2,1)S(1)}, u32[]{:S(2)}, u32[]{:S(2)}) %collective-permute-start.3) | collective-permute-done | bytes 2080 | tf_op jit(solution)/shard_map/ang_2/ppermute | solution.py:297
  16.1 0.0 collective-permute-done.4
  16.1 0.0 copy-done
  16.1 0.7 %fusion.1 = f32[8,256]{1,0:T(8,128)} fusion(bf16[128,256]{1,0:T(8,128)(2,1)S(1)} %bitcast.6, bf16[8,128]{1,0:T(8,128)(2,1)S(1)} %collective-permute-done.4, bf16[8,128]{1,0:T(8,128)(2,1)S(1)} %collective-permute-done.3, bf16[8,128]{1,0:T(8,128)(2,1)S(1)} %get-tuple-element.17, bf16[8,128]{1,0:T(8,128)(2,1)S(1)} %collective-permute-done.2), kind=kOutput, calls=%fused_computation.4 | convolution fusion | flops 527360 | bytes 81920 | tf_op jit(solution)/shard_map/dot_general | solution.py:299
  (1 shorter events, 0.0 us)
Async XLA Ops:
  0.0 16.1 %copy-start = (bf16[4,32,256]{2,1,0:T(8,128)(2,1)S(1)}, bf16[4,32,256]{2,1,0:T(8,128)(2,1)}, u32[]{:S(2)}) copy-start(bf16[4,32,256]{2,1,0:T(8,128)(2,1)} %param.8) | copy-start | bytes 196612
  0.0 6.1 %copy-start.1 = (bf16[688,256]{1,0:T(8,128)(2,1)S(1)}, bf16[688,256]{1,0:T(8,128)(2,1)}, u32[]{:S(2)}) copy-start(bf16[688,256]{1,0:T(8,128)(2,1)} %constant.14.clone.table) | copy-start | bytes 1056772
  1.0 5.1 %copy-start.2 = (s32[4,4]{1,0:T(4,128)S(1)}, s32[4,4]{1,0:T(4,128)}, u32[]{:S(2)}) copy-start(s32[4,4]{1,0:T(4,128)} %starts.1) | copy-start | bytes 196
  1.0 6.0 %collective-permute-start.1 = (bf16[4,2560]{1,0:T(4,128)(2,1)S(1)}, bf16[4,2560]{1,0:T(4,128)(2,1)S(1)}, u32[]{:S(2)}, u32[]{:S(2)}) collective-permute-start(bf16[4,2560]{1,0:T(4,128)(2,1)S(1)} %get-tuple-element.23), channel_id=1, source_target_pairs={{1,2},{2,1},{5,6},{6,5},{9,10},{10,9},{13,14},{14,13},{17,18},{18,... | collective-permute-start | bytes 61448 | tf_op jit(solution)/shard_map/hop_b/ppermute | solution.py:257
  1.7 5.4 %collective-permute-start = (bf16[4,2560]{1,0:T(4,128)(2,1)S(1)}, bf16[4,2560]{1,0:T(4,128)(2,1)S(1)}, u32[]{:S(2)}, u32[]{:S(2)}) collective-permute-start(bf16[4,2560]{1,0:T(4,128)(2,1)S(1)} %get-tuple-element.24), channel_id=1, source_target_pairs={{0,1},{2,3},{1,0},{3,2},{4,5},{6,7},{5,4},{7,6},{8,9},{10,11},{9,8... | collective-permute-start | bytes 61448 | tf_op jit(solution)/shard_map/hop_a/ppermute | solution.py:257
  8.0 5.4 %collective-permute-start.2 = (bf16[8,128]{1,0:T(8,128)(2,1)S(1)}, bf16[8,128]{1,0:T(8,128)(2,1)S(1)}, u32[]{:S(2)}, u32[]{:S(2)}) collective-permute-start(bf16[8,128]{1,0:T(8,128)(2,1)S(1)} %get-tuple-element.18), channel_id=1, source_target_pairs={{0,12},{4,8},{8,4},{12,0},{1,13},{5,9},{9,5},{13,1},{2,14},{6,10},... | collective-permute-start | bytes 6152 | tf_op jit(solution)/shard_map/ang_3/ppermute | solution.py:297
  11.6 4.5 %collective-permute-start.3 = (bf16[8,128]{1,0:T(8,128)(2,1)S(1)}, bf16[8,128]{1,0:T(8,128)(2,1)S(1)}, u32[]{:S(2)}, u32[]{:S(2)}) collective-permute-start(bf16[8,128]{1,0:T(8,128)(2,1)S(1)} %get-tuple-element.19), channel_id=1, source_target_pairs={{0,8},{4,12},{8,0},{12,4},{1,9},{5,13},{9,1},{13,5},{2,10},{6,14},... | collective-permute-start | bytes 6152 | tf_op jit(solution)/shard_map/ang_2/ppermute | solution.py:297
  11.6 4.5 %collective-permute-start.4 = (bf16[8,128]{1,0:T(8,128)(2,1)S(1)}, bf16[8,128]{1,0:T(8,128)(2,1)S(1)}, u32[]{:S(2)}, u32[]{:S(2)}) collective-permute-start(bf16[8,128]{1,0:T(8,128)(2,1)S(1)} %get-tuple-element.20), channel_id=1, source_target_pairs={{0,4},{4,0},{8,12},{12,8},{1,5},{5,1},{9,13},{13,9},{2,6},{6,2},{1... | collective-permute-start | bytes 6152 | tf_op jit(solution)/shard_map/ang_1/ppermute | solution.py:297
